TPU v7x, 32 devices: a whole 2x2x4 slice. The times are simulated.
32 devices in a mesh: gx: 4 (over y, x), gy: 8 (over z, core).
Axes of the slice: x: 2, y: 2, z: 4, core: 2. Of those that a mesh axis runs over, the one named last changes fastest.
Arguments:
- tokens: bfloat16 [4096, 8192], P('gy', 'gx'), may hold values from -6 to 6
- pair_ids: int32 [8], replicated, may hold values from 0 to 7, each once
- query_weight: bfloat16 [8192, 8192], P('gy', 'gx'), may hold values from -0.0625 to 0.0625
- key_matrix: bfloat16 [8192, 1024], P('gy', 'gx'), may hold values from -0.0625 to 0.0625
- value_matrix: bfloat16 [8192, 1024], P('gy', 'gx'), may hold values from -0.0625 to 0.0625
- query_bias: bfloat16 [8192], P('gx'), may hold values from -13 to 13
- key_bias: bfloat16 [1024], P('gx'), may hold values from -8 to 8
- value_offset_bias: bfloat16 [1024], P('gx'), may hold values from -3 to 3
Outputs:
- attn_out: bfloat16 [4096, 8192], P('gy', 'gx')
Inputs may be any that keep to these rules, and one draw needn't show every extreme that they name: `pair_ids`: each number from 0 to 7 appears once.
All inputs are finite; a program needn't handle non-finite values.
Results may differ from a plain program's by a relative error of at most 0.0055.
The roundings to bfloat16 on the way count: a program that leaves them out, or rounds other values in their place, can miss the bound.
Values may be sent and summed in bfloat16 or wider, within the bound.
A program may use at most 128 MiB of HBM per device.

v0:
```python
import math
import jax
import jax.numpy as jnp
from jax import lax
from jax.sharding import PartitionSpec as P

HEAD_SIZE = 128
rope_theta = 1000000.0
neg_large = -1e30


def table_lookup(entries, wanted):
    slot_ids = lax.iota(jnp.int32, entries.shape[0])
    return jnp.sum(jnp.where(wanted[:, None] == slot_ids[None, :], entries[None, :], 0), axis=1)


def layout_positions(pair_ids, total_row_count, tok_dev):
    half_len = tok_dev // 2
    row_ids = lax.iota(jnp.int32, total_row_count)
    within = row_ids % tok_dev
    owners = table_lookup(pair_ids, row_ids // tok_dev)
    mirrored = 2 * pair_ids.shape[0] - 1 - owners
    return jnp.where(
        within < half_len, owners * half_len + within, mirrored * half_len + within - half_len
    )


def apply_rotary(values, token_positions):
    half_size = values.shape[-1] // 2
    frequency = jnp.exp(
        lax.iota(jnp.float32, half_size) * (-2.0 * math.log(rope_theta) / values.shape[-1])
    )
    angles = token_positions.astype(jnp.float32)[:, None] * frequency[None, :]
    cos_part = jnp.cos(angles)[:, None, :]
    sin_part = jnp.sin(angles)[:, None, :]
    lower_half = values[..., :half_size]
    upper_half = values[..., half_size:]
    return jnp.concatenate(
        [
            lower_half * cos_part - upper_half * sin_part,
            upper_half * cos_part + lower_half * sin_part,
        ],
        axis=-1,
    )


def absorb(running, query_block, key_block, value_block, visible):
    row_peak, totals, outputs = running
    scale = 1.0 / math.sqrt(query_block.shape[-1])
    scores = (
        jnp.einsum("hqd,khd->hqk", query_block, key_block, preferred_element_type=jnp.float32)
        * scale
    )
    if visible is not None:
        scores = jnp.where(visible[None], scores, neg_large)
    new_peak = jnp.maximum(row_peak, jnp.max(scores, axis=-1))
    weights = jnp.exp(scores - new_peak[..., None])
    if visible is not None:
        weights = jnp.where(visible[None], weights, 0.0)
    rescale = jnp.exp(row_peak - new_peak)
    totals = totals * rescale + jnp.sum(weights, axis=-1)
    outputs = outputs * rescale[..., None] + jnp.einsum(
        "hqk,khd->hqd",
        weights.astype(jnp.bfloat16),
        value_block,
        preferred_element_type=jnp.float32,
    )
    return (new_peak, totals, outputs)


def on_device(
    tokens,
    pair_ids,
    query_weight,
    key_matrix,
    value_matrix,
    query_bias,
    key_bias,
    value_offset_bias,
):
    tok_dev = tokens.shape[0]
    half_len = tok_dev // 2
    whole_rows = tok_dev * lax.axis_size("gy")
    kv_local = key_matrix.shape[1] // HEAD_SIZE
    q_local = query_weight.shape[1] // HEAD_SIZE
    query_group_width = q_local // kv_local
    gathered = lax.all_gather(tokens, "gx", axis=1, tiled=True)
    stacked = jnp.concatenate([query_weight, key_matrix, value_matrix], axis=1)
    projected = jnp.dot(
        gathered,
        lax.all_gather(stacked, "gy", axis=0, tiled=True),
        preferred_element_type=jnp.float32,
    )
    all_positions = layout_positions(pair_ids, whole_rows, tok_dev)
    own_index = lax.axis_index("gy")
    own_positions = lax.dynamic_slice_in_dim(all_positions, own_index * tok_dev, tok_dev, 0)
    own_pair = table_lookup(pair_ids, jnp.reshape(own_index, (1,)))[0]
    q_cols = q_local * HEAD_SIZE
    kv_cols = kv_local * HEAD_SIZE
    queries = projected[:, :q_cols] + query_bias.astype(jnp.float32)
    queries = apply_rotary(queries.reshape(tok_dev, q_local, HEAD_SIZE), own_positions).astype(
        jnp.bfloat16
    )
    projected_key_rows = projected[:, q_cols : q_cols + kv_cols] + key_bias.astype(jnp.float32)
    projected_key_rows = (
        apply_rotary(projected_key_rows.reshape(tok_dev, kv_local, HEAD_SIZE), own_positions)
        .astype(jnp.bfloat16)
        .reshape(tok_dev, kv_cols)
    )
    projected_value_rows = (
        projected[:, q_cols + kv_cols :] + value_offset_bias.astype(jnp.float32)
    ).astype(jnp.bfloat16)
    query_rows = (
        queries.reshape(tok_dev, kv_local, query_group_width, HEAD_SIZE)
        .transpose(1, 0, 2, 3)
        .reshape(kv_local, tok_dev * query_group_width, HEAD_SIZE)
    )
    row_positions = jnp.repeat(own_positions, query_group_width)
    row_total = tok_dev * query_group_width
    initial = (
        jnp.full((kv_local, row_total), neg_large, jnp.float32),
        jnp.zeros((kv_local, row_total), jnp.float32),
        jnp.zeros((kv_local, row_total, HEAD_SIZE), jnp.float32),
    )

    def paired(running, key_shard, value_shard, earlier):
        cut_rows = half_len * query_group_width
        former = tuple((member[:, :cut_rows] for member in running))
        latter = tuple((member[:, cut_rows:] for member in running))
        query_former = query_rows[:, :cut_rows]
        query_latter = query_rows[:, cut_rows:]
        latter = absorb(latter, query_latter, key_shard[:half_len], value_shard[:half_len], None)
        picked_state = tuple(
            (jnp.where(earlier, left, right) for left, right in zip(former, latter))
        )
        query_pick = jnp.where(earlier, query_former, query_latter)
        key_pick = jnp.where(earlier, key_shard[:half_len], key_shard[half_len:])
        value_pick = jnp.where(earlier, value_shard[:half_len], value_shard[half_len:])
        updated = absorb(picked_state, query_pick, key_pick, value_pick, None)
        former = tuple((jnp.where(earlier, fresh, kept) for fresh, kept in zip(updated, former)))
        latter = tuple((jnp.where(earlier, kept, fresh) for fresh, kept in zip(updated, latter)))
        return tuple(
            (jnp.concatenate([left, right], axis=1) for left, right in zip(former, latter))
        )

    key_piece = lax.all_gather(projected_key_rows, "gy", axis=0, tiled=True)
    value_piece = lax.all_gather(projected_value_rows, "gy", axis=0, tiled=True)
    total_row_count = key_piece.shape[0]

    def one_shard(shard_index, carried):
        begin = shard_index * tok_dev
        key_shard = lax.dynamic_slice_in_dim(key_piece, begin, tok_dev, 0).reshape(
            tok_dev, kv_local, HEAD_SIZE
        )
        value_shard = lax.dynamic_slice_in_dim(value_piece, begin, tok_dev, 0).reshape(
            tok_dev, kv_local, HEAD_SIZE
        )
        source = jnp.reshape(begin // tok_dev, (1,))
        their_pair = table_lookup(pair_ids, source)[0]

        def itself(state_in):
            key_positions = lax.dynamic_slice_in_dim(all_positions, begin, tok_dev, 0)
            visible = key_positions[None, :] <= row_positions[:, None]
            return absorb(state_in, query_rows, key_shard, value_shard, visible)

        def elsewhere(state_in):
            return paired(state_in, key_shard, value_shard, their_pair < own_pair)

        return lax.cond(their_pair == own_pair, itself, elsewhere, carried)

    row_peak, totals, outputs = lax.fori_loop(0, total_row_count // tok_dev, one_shard, initial)
    normalized = (outputs / totals[..., None]).astype(jnp.bfloat16)
    return (
        normalized.reshape(kv_local, tok_dev, query_group_width, HEAD_SIZE)
        .transpose(1, 0, 2, 3)
        .reshape(tok_dev, q_cols)
    )


def solution(mesh):
    in_specs = (
        P("gy", "gx"),
        P(),
        P("gy", "gx"),
        P("gy", "gx"),
        P("gy", "gx"),
        P("gx"),
        P("gx"),
        P("gx"),
    )
    out_specs = P("gy", "gx")
    return jax.shard_map(
        on_device, mesh=mesh, in_specs=in_specs, out_specs=out_specs, check_vma=False
    )
```

profile of v0, /device:TPU:0, one launch (start us, length us, event | category | flops | bytes accessed | tf_op | source)
XLA Modules:
  0.0 768.3 jit_solution(7641844237663635094)
XLA Ops:
  7.3 6.9 pad_maximum_fusion.3
  15.7 83.8 %all-gather.7.cloned.1.call-done = bf16[512,8192]{1,0:T(8,128)(2,1)} async-done(((bf16[512,2048]{1,0:T(8,128)(2,1)}), bf16[512,8192]{1,0:T(8,128)(2,1)}) %all-gather.7.cloned.1.call-update) | async-done | bytes 8388624 | tf_op jit(solution)/shard_map/all_gather | solution.py:87
  99.4 360.5 %all-gather.5.cloned.1.call-done = bf16[8192,2560]{1,0:T(8,128)(2,1)} async-done(((bf16[1024,2560]{1,0:T(8,128)(2,1)}), bf16[8192,2560]{1,0:T(8,128)(2,1)}) %all-gather.5.cloned.1.call-update) | async-done | bytes 41943056 | tf_op jit(solution)/shard_map/all_gather | solution.py:91
  459.9 30.0 %convolution_bitcast_fusion = f32[512,2560]{0,1:T(8,128)} fusion(bf16[8192,2560]{1,0:T(8,128)(2,1)} %all-gather.5.cloned.1.call-done, bf16[512,8192]{1,0:T(8,128)(2,1)} %all-gather.7.cloned.1.call-done), kind=kOutput, calls=%fused_computation.67 | convolution fusion | flops 21474836480 | bytes 55574528 | tf_op jit(solution)/shard_map/dot_general | solution.py:89
  503.4 4.1 maximum_bitcast_fusion
  507.5 13.1 %all-gather.9.cloned.1.call-done = bf16[4096,256]{0,1:T(8,128)(2,1)} async-done(((bf16[512,256]{0,1:T(8,128)(2,1)}), bf16[4096,256]{0,1:T(8,128)(2,1)}) %all-gather.9.cloned.1.call-update) | async-done | bytes 2097168 | tf_op jit(solution)/shard_map/all_gather | solution.py:146
  520.6 30.0 %all-gather.11.cloned.1.call-done = bf16[4096,256]{0,1:T(8,128)(2,1)} async-done(((bf16[512,256]{0,1:T(8,128)(2,1)}), bf16[4096,256]{0,1:T(8,128)(2,1)}) %all-gather.11.cloned.1.call-update) | async-done | bytes 2097168 | tf_op jit(solution)/shard_map/all_gather | solution.py:147
  553.5 203.1 %while.20 = (s32[]{:T(128)}, f32[2,4096]{1,0:T(2,128)S(1)}, f32[2,4096]{1,0:T(2,128)}, f32[2,4096,128]{2,1,0:T(8,128)}, s32[8]{0:T(128)S(1)}, /*index=5*/s32[]{:...) while((s32[]{:T(128)}, f32[2,4096]{1,0:T(2,128)S(1)}, ...), condition=%wide.region_12.13_spmd.clone, body=%wide.region_2.12_spmd.clone.sunk | while | flops 2206220288 | bytes 138748624 | solution.py:171
  556.6 28.6 %conditional.3 = (f32[2,4096]{1,0:T(2,128)}, f32[2,4096]{1,0:T(2,128)}, f32[2,4096,128]{2,1,0:T(8,128)}) conditional(s32[]{:T(128)} %convert_element_type.69, (s32[]{:T(128)}, s32[]{:T(128)}, f32[2,4096]{1,0:T(2,128)S(1)}, bf16[2,4096,128]{2,1,0:T(8,128)(2,1)}, bf16[512,2,128]{0,2,1:T(8,128)(2,1)S(1)}, /*index=5*/f32[2,4096]{1,0:T(2,128)}, ...), branch_computations={%region_4.8_spmd, %region_9.11_spmd} | conditional | flops 2206220288 | bytes 137633952 | solution.py:169
  558.3 5.8 fusion.28
  566.1 5.3 fusion.30
  572.9 12.3 %fusion.34 = f32[2,4096,128]{2,1,0:T(8,128)} fusion(bf16[512,2,128]{0,2,1:T(8,128)(2,1)S(1)} %get-tuple-element.414, f32[2,4096,512]{1,2,0:T(8,128)} %copy-done.3, f32[2,4096]{1,0:T(2,128)} %max.8, pred[4096,512]{0,1:T(8,128)(4,1)S(1)} %broadcast_compare_fusion, f32[2,4096,128]{2,1,0:T(8,128)} %get-tuple-element.321, f32[2,4096]{1,0:T(2,128)S(1)} %get-tuple-element.446), kind=kOutput, calls=%fused_computation.55 | convolution fusion | flops 1096810496 | bytes 27590656 | tf_op jit(solution)/shard_map/while/body/eval_jaxpr/cond/branch_1_fun/hqk,khd->hqd/dot_general | solution.py:62
  589.0 20.6 %conditional.3 = (f32[2,4096]{1,0:T(2,128)}, f32[2,4096]{1,0:T(2,128)}, f32[2,4096,128]{2,1,0:T(8,128)}) conditional(s32[]{:T(128)} %convert_element_type.69, (s32[]{:T(128)}, s32[]{:T(128)}, f32[2,4096]{1,0:T(2,128)S(1)}, bf16[2,4096,128]{2,1,0:T(8,128)(2,1)}, bf16[512,2,128]{0,2,1:T(8,128)(2,1)S(1)}, /*index=5*/f32[2,4096]{1,0:T(2,128)}, ...), branch_computations={%region_4.8_spmd, %region_9.11_spmd} | conditional | flops 2206220288 | bytes 137633952 | solution.py:169
  598.4 4.4 convolution_add_fusion.1
  613.4 20.6 %conditional.3 = (f32[2,4096]{1,0:T(2,128)}, f32[2,4096]{1,0:T(2,128)}, f32[2,4096,128]{2,1,0:T(8,128)}) conditional(s32[]{:T(128)} %convert_element_type.69, (s32[]{:T(128)}, s32[]{:T(128)}, f32[2,4096]{1,0:T(2,128)S(1)}, bf16[2,4096,128]{2,1,0:T(8,128)(2,1)}, bf16[512,2,128]{0,2,1:T(8,128)(2,1)S(1)}, /*index=5*/f32[2,4096]{1,0:T(2,128)}, ...), branch_computations={%region_4.8_spmd, %region_9.11_spmd} | conditional | flops 2206220288 | bytes 137633952 | solution.py:169
  617.1 2.8 multiply_reduce_fusion.1
  622.8 4.4 convolution_add_fusion.1
  637.8 20.6 %conditional.3 = (f32[2,4096]{1,0:T(2,128)}, f32[2,4096]{1,0:T(2,128)}, f32[2,4096,128]{2,1,0:T(8,128)}) conditional(s32[]{:T(128)} %convert_element_type.69, (s32[]{:T(128)}, s32[]{:T(128)}, f32[2,4096]{1,0:T(2,128)S(1)}, bf16[2,4096,128]{2,1,0:T(8,128)(2,1)}, bf16[512,2,128]{0,2,1:T(8,128)(2,1)S(1)}, /*index=5*/f32[2,4096]{1,0:T(2,128)}, ...), branch_computations={%region_4.8_spmd, %region_9.11_spmd} | conditional | flops 2206220288 | bytes 137633952 | solution.py:169
  641.5 2.8 multiply_reduce_fusion.1
  647.2 4.4 convolution_add_fusion.1
  662.2 20.6 %conditional.3 = (f32[2,4096]{1,0:T(2,128)}, f32[2,4096]{1,0:T(2,128)}, f32[2,4096,128]{2,1,0:T(8,128)}) conditional(s32[]{:T(128)} %convert_element_type.69, (s32[]{:T(128)}, s32[]{:T(128)}, f32[2,4096]{1,0:T(2,128)S(1)}, bf16[2,4096,128]{2,1,0:T(8,128)(2,1)}, bf16[512,2,128]{0,2,1:T(8,128)(2,1)S(1)}, /*index=5*/f32[2,4096]{1,0:T(2,128)}, ...), branch_computations={%region_4.8_spmd, %region_9.11_spmd} | conditional | flops 2206220288 | bytes 137633952 | solution.py:169
  665.9 2.8 multiply_reduce_fusion.1
  671.6 4.4 convolution_add_fusion.1
  686.6 20.6 %conditional.3 = (f32[2,4096]{1,0:T(2,128)}, f32[2,4096]{1,0:T(2,128)}, f32[2,4096,128]{2,1,0:T(8,128)}) conditional(s32[]{:T(128)} %convert_element_type.69, (s32[]{:T(128)}, s32[]{:T(128)}, f32[2,4096]{1,0:T(2,128)S(1)}, bf16[2,4096,128]{2,1,0:T(8,128)(2,1)}, bf16[512,2,128]{0,2,1:T(8,128)(2,1)S(1)}, /*index=5*/f32[2,4096]{1,0:T(2,128)}, ...), branch_computations={%region_4.8_spmd, %region_9.11_spmd} | conditional | flops 2206220288 | bytes 137633952 | solution.py:169
  690.3 2.8 multiply_reduce_fusion.1
  696.0 4.4 convolution_add_fusion.1
  710.9 20.6 %conditional.3 = (f32[2,4096]{1,0:T(2,128)}, f32[2,4096]{1,0:T(2,128)}, f32[2,4096,128]{2,1,0:T(8,128)}) conditional(s32[]{:T(128)} %convert_element_type.69, (s32[]{:T(128)}, s32[]{:T(128)}, f32[2,4096]{1,0:T(2,128)S(1)}, bf16[2,4096,128]{2,1,0:T(8,128)(2,1)}, bf16[512,2,128]{0,2,1:T(8,128)(2,1)S(1)}, /*index=5*/f32[2,4096]{1,0:T(2,128)}, ...), branch_computations={%region_4.8_spmd, %region_9.11_spmd} | conditional | flops 2206220288 | bytes 137633952 | solution.py:169
  720.4 4.4 convolution_add_fusion.1
  735.3 20.6 %conditional.3 = (f32[2,4096]{1,0:T(2,128)}, f32[2,4096]{1,0:T(2,128)}, f32[2,4096,128]{2,1,0:T(8,128)}) conditional(s32[]{:T(128)} %convert_element_type.69, (s32[]{:T(128)}, s32[]{:T(128)}, f32[2,4096]{1,0:T(2,128)S(1)}, bf16[2,4096,128]{2,1,0:T(8,128)(2,1)}, bf16[512,2,128]{0,2,1:T(8,128)(2,1)S(1)}, /*index=5*/f32[2,4096]{1,0:T(2,128)}, ...), branch_computations={%region_4.8_spmd, %region_9.11_spmd} | conditional | flops 2206220288 | bytes 137633952 | solution.py:169
  739.1 2.8 multiply_reduce_fusion.1
  744.8 4.4 convolution_add_fusion.1
  756.7 2.9 fusion.41
  (209 shorter events, 136.1 us)
Async XLA Ops:
  6.5 92.9 %all-gather.7.cloned.1.call-start = ((), (), s32[]{:S(2)}) async-start(), calls=%async_computation.1 | async-start | bytes 10485760 | tf_op jit(solution)/shard_map/all_gather | solution.py:87
  7.3 452.7 %all-gather.5.cloned.1.call-start = ((), (), s32[]{:S(2)}) async-start(), calls=%async_computation | async-start | bytes 47185920 | tf_op jit(solution)/shard_map/all_gather | solution.py:91
  14.2 506.4 %all-gather.9.cloned.1.call-start = ((), (), s32[]{:S(2)}) async-start(), calls=%async_computation.2 | async-start | bytes 2359296 | tf_op jit(solution)/shard_map/all_gather | solution.py:146
  15.6 477.7 %copy-start.7 = (bf16[2048]{0:T(1024)(128)(2,1)S(1)}, bf16[2048]{0:T(1024)(128)(2,1)}, u32[]{:S(2)}) copy-start(bf16[2048]{0:T(1024)(128)(2,1)} %param.17) | copy-start | bytes 12292
  492.8 57.9 %all-gather.11.cloned.1.call-start = ((), (), s32[]{:S(2)}) async-start(), calls=%async_computation.3 | async-start | bytes 2359296 | tf_op jit(solution)/shard_map/all_gather | solution.py:147
  564.2 7.2 copy-start.3
  566.1 5.3 copy-start.6
  592.7 4.3 copy-start
  595.5 2.0 copy-start.2
  598.4 4.4 copy-start.1
  598.4 5.3 copy-start.4
  617.1 4.3 copy-start
  619.9 2.0 copy-start.2
  622.8 4.4 copy-start.1
  622.8 5.3 copy-start.4
  641.5 4.3 copy-start
  644.3 2.0 copy-start.2
  647.2 4.4 copy-start.1
  647.2 5.3 copy-start.4
  665.9 4.3 copy-start
  668.6 2.0 copy-start.2
  671.6 4.4 copy-start.1
  671.6 5.3 copy-start.4
  690.3 4.3 copy-start
  696.0 4.4 copy-start.1
  696.0 5.3 copy-start.4
  714.7 4.3 copy-start
  720.4 4.4 copy-start.1
  720.4 5.3 copy-start.4
  739.0 4.3 copy-start
  744.8 4.4 copy-start.1
  744.8 5.3 copy-start.4
  (7 other events, 9.6 us)
Sparse Core Ops, SparseCore 0:
  9.2 90.1 all-gather.6
  101.1 358.8 all-gather.4
  492.9 27.7 all-gather.8
  522.1 28.5 all-gather.10
where the time goes:
time: 771 us; the launch traced here: 768 us
  waiting for transfers between devices  489 us (63%)
  matrix products  126 us (16%)
  other arithmetic  83.3 us (11%)
  local copies, waits for them, and re-layouts  37.8 us (5%)
  loops' own time  19.6 us (3%)
  between operations  13.2 us (2%)
    all_gather x1, waiting for transfers between devices, on_device(): lax.all_gather(stacked, 'gy', axis=0, tiled=True)  361 us
    all_gather x1, waiting for transfers between devices, on_device(): gathered = lax.all_gather(tokens, 'gx', axis=1, tiled=True)  83.8 us
    dot_general x15, matrix products, absorb(): jnp.einsum('hqk,khd->hqd', weights.astype(jnp.bfloat16), value_block, pre...  54.5 us
    dot_general x15, matrix products, absorb(): jnp.einsum('hqd,khd->hqk', query_block, key_block, preferred_element_type...  41.1 us
    all_gather x1, waiting for transfers between devices, on_device(): value_piece = lax.all_gather(projected_value_rows, 'gy', axis=0, tiled=True)  30 us
    dot_general x1, matrix products, on_device(): jnp.dot(gathered, lax.all_gather(stacked, 'gy', axis=0, tiled=True), pref...  30 us
    concatenate x21, other arithmetic, paired(): jnp.concatenate([left, right], axis=1)  24.3 us
    reduce_sum x8, other arithmetic, absorb(): totals = totals * rescale + jnp.sum(weights, axis=-1)  15.5 us
  transfers between devices with their start and end apart: 4, of which 4 were waited for; matrix products, arithmetic and copies ran while one was open for 3% of the time, Pallas kernels for 0%

commit v1 on v0

--- a/solution.py
+++ b/solution.py
@@ -84,7 +84,12 @@
     kv_local = key_matrix.shape[1] // HEAD_SIZE
     q_local = query_weight.shape[1] // HEAD_SIZE
     query_group_width = q_local // kv_local
-    gathered = lax.all_gather(tokens, "gx", axis=1, tiled=True)
+    ring = [tokens]
+    for hop in range(3):
+        ring.append(lax.ppermute(ring[-1], "gx", [(dev, (dev + 1) % 4) for dev in range(4)]))
+    gathered = jnp.roll(
+        jnp.concatenate(ring[::-1], axis=1), (lax.axis_index("gx") + 1) * ring[0].shape[1], axis=1
+    )
     stacked = jnp.concatenate([query_weight, key_matrix, value_matrix], axis=1)
     projected = jnp.dot(
         gathered,

time: 771 us -> 696 us (0.903)
  waiting for transfers between devices: 489 us -> 385 us
  local copies, waits for them, and re-layouts: 37.8 us -> 65.6 us
    all_gather x1, waiting for transfers between devices: 361 us -> 196 us  [on_device(): lax.all_gather(stacked, 'gy', axis=0, tiled=True)]
    ppermute x0 -> x3, waiting for transfers between devices: none -> 140 us  [on_device(): lax.ppermute(ring[-1], 'gx', [(dev, (dev + 1) % 4) for dev in range(4)])]
    all_gather x1 -> x0, waiting for transfers between devices: 83.8 us -> none  [on_device(): gathered = lax.all_gather(tokens, 'gx', axis=1, tiled=True)]
    unnamed x9 -> x25, local copies, waits for them, and re-layouts: 2.45 us -> 24.7 us
    dynamic_slice x0 -> x8, local copies, waits for them, and re-layouts: none -> 7.8 us  [one_shard(): lax.dynamic_slice_in_dim(key_piece, begin, tok_dev, 0)]
  transfers between devices with their start and end apart: 4 -> 6, of which waited for: 4 -> 6; matrix products, arithmetic and copies ran while one was open for 3% -> 4% of each run, Pallas kernels for 0% -> 0%
where the time goes in v1:
time: 696 us; the launch traced here: 693 us
  waiting for transfers between devices  385 us (55%)
  matrix products  123 us (18%)
  other arithmetic  81.1 us (12%)
  local copies, waits for them, and re-layouts  65.6 us (9%)
  loops' own time  20.8 us (3%)
  between operations  13.3 us (2%)
    all_gather x1, waiting for transfers between devices, on_device(): lax.all_gather(stacked, 'gy', axis=0, tiled=True)  196 us
    ppermute x3, waiting for transfers between devices, on_device(): lax.ppermute(ring[-1], 'gx', [(dev, (dev + 1) % 4) for dev in range(4)])  140 us
    dot_general x15, matrix products, absorb(): jnp.einsum('hqk,khd->hqd', weights.astype(jnp.bfloat16), value_block, pre...  54.5 us
    dot_general x15, matrix products, absorb(): jnp.einsum('hqd,khd->hqk', query_block, key_block, preferred_element_type...  41.1 us
    all_gather x1, waiting for transfers between devices, on_device(): value_piece = lax.all_gather(projected_value_rows, 'gy', axis=0, tiled=True)  30.2 us
    dot_general x1, matrix products, on_device(): jnp.dot(gathered, lax.all_gather(stacked, 'gy', axis=0, tiled=True), pref...  27 us
    unnamed x25, local copies, waits for them, and re-layouts  24.7 us
    concatenate x21, other arithmetic, paired(): jnp.concatenate([left, right], axis=1)  24.2 us
  transfers between devices with their start and end apart: 6, of which 6 were waited for; matrix products, arithmetic and copies ran while one was open for 4% of the time, Pallas kernels for 0%

profile of v1, /device:TPU:0, one launch (start us, length us, event | category | flops | bytes accessed | tf_op | source)
XLA Modules:
  0.0 692.6 jit_solution(106286395317263812)
XLA Ops:
  6.5 6.9 pad_maximum_fusion.3
  15.0 3.0 collective-permute-start
  18.0 46.6 %collective-permute-done = bf16[512,2048]{1,0:T(8,128)(2,1)S(1)} collective-permute-done((bf16[512,2048]{1,0:T(8,128)(2,1)S(1)}, bf16[512,2048]{1,0:T(8,128)(2,1)S(1)}, u32[]{:S(2)}, u32[]{:S(2)}) %collective-permute-start) | collective-permute-done | bytes 2097184 | tf_op jit(solution)/shard_map/ppermute | solution.py:89
  66.7 47.1 %collective-permute-done.1 = bf16[512,2048]{1,0:T(8,128)(2,1)} collective-permute-done((bf16[512,2048]{1,0:T(8,128)(2,1)S(1)}, bf16[512,2048]{1,0:T(8,128)(2,1)}, u32[]{:S(2)}, u32[]{:S(2)}) %collective-permute-start.1) | collective-permute-done | bytes 2097184 | tf_op jit(solution)/shard_map/ppermute | solution.py:89
  115.1 46.0 %collective-permute-done.2 = bf16[512,2048]{1,0:T(8,128)(2,1)} collective-permute-done((bf16[512,2048]{1,0:T(8,128)(2,1)}, bf16[512,2048]{1,0:T(8,128)(2,1)}, u32[]{:S(2)}, u32[]{:S(2)}) %collective-permute-start.2) | collective-permute-done | bytes 2097184 | tf_op jit(solution)/shard_map/ppermute | solution.py:89
  161.1 3.2 constant_dynamic-update-slice_fusion.7
  164.3 3.1 constant_dynamic-update-slice_fusion.6
  170.2 3.1 constant_dynamic-update-slice_fusion.3
  173.3 3.1 constant_dynamic-update-slice_fusion.2
  179.3 195.9 %all-gather.4.cloned.1.call-done = bf16[8192,2560]{1,0:T(8,128)(2,1)} async-done(((bf16[1024,2560]{1,0:T(8,128)(2,1)}), bf16[8192,2560]{1,0:T(8,128)(2,1)}) %all-gather.4.cloned.1.call-update) | async-done | bytes 41943056 | tf_op jit(solution)/shard_map/all_gather | solution.py:96
  375.2 27.0 %fusion.41 = f32[512,2560]{1,0:T(8,128)S(1)} fusion(bf16[8192,2560]{1,0:T(8,128)(2,1)} %all-gather.4.cloned.1.call-done, bf16[512,16384]{1,0:T(8,128)(2,1)} %constant_dynamic-update-slice_fusion, s32[]{:T(128)S(6)} %select_n.157), kind=kOutput, calls=%fused_computation.66 | convolution fusion | flops 21474836480 | bytes 55574532 | tf_op jit(solution)/shard_map/dot_general | solution.py:94
  417.1 18.8 %all-gather.6.cloned.1.call-done = bf16[4096,256]{0,1:T(8,128)(2,1)} async-done(((bf16[512,256]{0,1:T(8,128)(2,1)}), bf16[4096,256]{0,1:T(8,128)(2,1)}) %all-gather.6.cloned.1.call-update) | async-done | bytes 2097168 | tf_op jit(solution)/shard_map/all_gather | solution.py:151
  435.9 30.2 %all-gather.8.cloned.1.call-done = bf16[4096,256]{1,0:T(8,128)(2,1)} async-done(((bf16[512,256]{1,0:T(8,128)(2,1)}), bf16[4096,256]{1,0:T(8,128)(2,1)}) %all-gather.8.cloned.1.call-update) | async-done | bytes 2097168 | tf_op jit(solution)/shard_map/all_gather | solution.py:152
  468.9 212.0 %while.20 = (s32[]{:T(128)}, f32[2,4096]{1,0:T(2,128)S(1)}, f32[2,4096]{1,0:T(2,128)}, f32[2,4096,128]{2,1,0:T(8,128)}, s32[8]{0:T(128)S(1)}, /*index=5*/s32[]{:...) while((s32[]{:T(128)}, f32[2,4096]{1,0:T(2,128)S(1)}, ...), condition=%wide.region_12.13_spmd.clone, body=%wide.region_2.12_spmd.clone.sunk | while | flops 2206220288 | bytes 139272912 | solution.py:176
  473.0 28.6 %conditional.3 = (f32[2,4096]{1,0:T(2,128)}, f32[2,4096]{1,0:T(2,128)}, f32[2,4096,128]{2,1,0:T(8,128)}) conditional(s32[]{:T(128)} %convert_element_type.69, (s32[]{:T(128)}, s32[]{:T(128)}, f32[2,4096]{1,0:T(2,128)S(1)}, bf16[2,4096,128]{2,1,0:T(8,128)(2,1)}, bf16[512,2,128]{0,2,1:T(8,128)(2,1)S(1)}, /*index=5*/f32[2,4096]{1,0:T(2,128)}, ...), branch_computations={%region_4.8_spmd, %region_9.11_spmd} | conditional | flops 2206220288 | bytes 137633952 | solution.py:174
  474.7 5.8 fusion.28
  482.5 5.3 fusion.30
  489.3 12.4 %fusion.34 = f32[2,4096,128]{2,1,0:T(8,128)} fusion(bf16[512,2,128]{0,2,1:T(8,128)(2,1)S(1)} %get-tuple-element.414, f32[2,4096,512]{1,2,0:T(8,128)} %copy-done.3, f32[2,4096]{1,0:T(2,128)} %max.8, pred[4096,512]{0,1:T(8,128)(4,1)S(1)} %broadcast_compare_fusion, f32[2,4096,128]{2,1,0:T(8,128)} %get-tuple-element.321, f32[2,4096]{1,0:T(2,128)S(1)} %get-tuple-element.457), kind=kOutput, calls=%fused_computation.55 | convolution fusion | flops 1096810496 | bytes 27590656 | tf_op jit(solution)/shard_map/while/body/eval_jaxpr/cond/branch_1_fun/hqk,khd->hqd/dot_general | solution.py:62
  506.5 20.7 %conditional.3 = (f32[2,4096]{1,0:T(2,128)}, f32[2,4096]{1,0:T(2,128)}, f32[2,4096,128]{2,1,0:T(8,128)}) conditional(s32[]{:T(128)} %convert_element_type.69, (s32[]{:T(128)}, s32[]{:T(128)}, f32[2,4096]{1,0:T(2,128)S(1)}, bf16[2,4096,128]{2,1,0:T(8,128)(2,1)}, bf16[512,2,128]{0,2,1:T(8,128)(2,1)S(1)}, /*index=5*/f32[2,4096]{1,0:T(2,128)}, ...), branch_computations={%region_4.8_spmd, %region_9.11_spmd} | conditional | flops 2206220288 | bytes 137633952 | solution.py:174
  516.0 4.4 convolution_add_fusion.1
  532.0 20.7 %conditional.3 = (f32[2,4096]{1,0:T(2,128)}, f32[2,4096]{1,0:T(2,128)}, f32[2,4096,128]{2,1,0:T(8,128)}) conditional(s32[]{:T(128)} %convert_element_type.69, (s32[]{:T(128)}, s32[]{:T(128)}, f32[2,4096]{1,0:T(2,128)S(1)}, bf16[2,4096,128]{2,1,0:T(8,128)(2,1)}, bf16[512,2,128]{0,2,1:T(8,128)(2,1)S(1)}, /*index=5*/f32[2,4096]{1,0:T(2,128)}, ...), branch_computations={%region_4.8_spmd, %region_9.11_spmd} | conditional | flops 2206220288 | bytes 137633952 | solution.py:174
  541.5 4.4 convolution_add_fusion.1
  557.5 20.7 %conditional.3 = (f32[2,4096]{1,0:T(2,128)}, f32[2,4096]{1,0:T(2,128)}, f32[2,4096,128]{2,1,0:T(8,128)}) conditional(s32[]{:T(128)} %convert_element_type.69, (s32[]{:T(128)}, s32[]{:T(128)}, f32[2,4096]{1,0:T(2,128)S(1)}, bf16[2,4096,128]{2,1,0:T(8,128)(2,1)}, bf16[512,2,128]{0,2,1:T(8,128)(2,1)S(1)}, /*index=5*/f32[2,4096]{1,0:T(2,128)}, ...), branch_computations={%region_4.8_spmd, %region_9.11_spmd} | conditional | flops 2206220288 | bytes 137633952 | solution.py:174
  567.0 4.4 convolution_add_fusion.1
  583.0 20.7 %conditional.3 = (f32[2,4096]{1,0:T(2,128)}, f32[2,4096]{1,0:T(2,128)}, f32[2,4096,128]{2,1,0:T(8,128)}) conditional(s32[]{:T(128)} %convert_element_type.69, (s32[]{:T(128)}, s32[]{:T(128)}, f32[2,4096]{1,0:T(2,128)S(1)}, bf16[2,4096,128]{2,1,0:T(8,128)(2,1)}, bf16[512,2,128]{0,2,1:T(8,128)(2,1)S(1)}, /*index=5*/f32[2,4096]{1,0:T(2,128)}, ...), branch_computations={%region_4.8_spmd, %region_9.11_spmd} | conditional | flops 2206220288 | bytes 137633952 | solution.py:174
  592.5 4.4 convolution_add_fusion.1
  608.5 20.7 %conditional.3 = (f32[2,4096]{1,0:T(2,128)}, f32[2,4096]{1,0:T(2,128)}, f32[2,4096,128]{2,1,0:T(8,128)}) conditional(s32[]{:T(128)} %convert_element_type.69, (s32[]{:T(128)}, s32[]{:T(128)}, f32[2,4096]{1,0:T(2,128)S(1)}, bf16[2,4096,128]{2,1,0:T(8,128)(2,1)}, bf16[512,2,128]{0,2,1:T(8,128)(2,1)S(1)}, /*index=5*/f32[2,4096]{1,0:T(2,128)}, ...), branch_computations={%region_4.8_spmd, %region_9.11_spmd} | conditional | flops 2206220288 | bytes 137633952 | solution.py:174
  618.0 4.4 convolution_add_fusion.1
  634.0 20.7 %conditional.3 = (f32[2,4096]{1,0:T(2,128)}, f32[2,4096]{1,0:T(2,128)}, f32[2,4096,128]{2,1,0:T(8,128)}) conditional(s32[]{:T(128)} %convert_element_type.69, (s32[]{:T(128)}, s32[]{:T(128)}, f32[2,4096]{1,0:T(2,128)S(1)}, bf16[2,4096,128]{2,1,0:T(8,128)(2,1)}, bf16[512,2,128]{0,2,1:T(8,128)(2,1)S(1)}, /*index=5*/f32[2,4096]{1,0:T(2,128)}, ...), branch_computations={%region_4.8_spmd, %region_9.11_spmd} | conditional | flops 2206220288 | bytes 137633952 | solution.py:174
  643.5 4.4 convolution_add_fusion.1
  659.5 20.7 %conditional.3 = (f32[2,4096]{1,0:T(2,128)}, f32[2,4096]{1,0:T(2,128)}, f32[2,4096,128]{2,1,0:T(8,128)}) conditional(s32[]{:T(128)} %convert_element_type.69, (s32[]{:T(128)}, s32[]{:T(128)}, f32[2,4096]{1,0:T(2,128)S(1)}, bf16[2,4096,128]{2,1,0:T(8,128)(2,1)}, bf16[512,2,128]{0,2,1:T(8,128)(2,1)S(1)}, /*index=5*/f32[2,4096]{1,0:T(2,128)}, ...), branch_computations={%region_4.8_spmd, %region_9.11_spmd} | conditional | flops 2206220288 | bytes 137633952 | solution.py:174
  669.0 4.4 convolution_add_fusion.1
  (245 shorter events, 170.2 us)
Async XLA Ops:
  6.5 368.7 %all-gather.4.cloned.1.call-start = ((), (), s32[]{:S(2)}) async-start(), calls=%async_computation | async-start | bytes 47185920 | tf_op jit(solution)/shard_map/all_gather | solution.py:96
  13.4 100.4 %copy-start.13 = (bf16[256]{0:T(256)(128)(2,1)S(1)}, bf16[256]{0:T(256)(128)(2,1)}, u32[]{:S(2)}) copy-start(bf16[256]{0:T(256)(128)(2,1)} %param.18) | copy-start | bytes 1540
  13.4 100.4 %copy-start.14 = (bf16[256]{0:T(256)(128)(2,1)S(1)}, bf16[256]{0:T(256)(128)(2,1)}, u32[]{:S(2)}) copy-start(bf16[256]{0:T(256)(128)(2,1)} %param.19) | copy-start | bytes 1540
  13.4 100.4 %copy-start.12 = (s32[8]{0:T(128)S(1)}, s32[8]{0:T(128)}, u32[]{:S(2)}) copy-start(s32[8]{0:T(128)} %param.13) | copy-start | bytes 100
  13.5 422.4 %all-gather.6.cloned.1.call-start = ((), (), s32[]{:S(2)}) async-start(), calls=%async_computation.1 | async-start | bytes 2359296 | tf_op jit(solution)/shard_map/all_gather | solution.py:151
  15.0 49.5 %collective-permute-start = (bf16[512,2048]{1,0:T(8,128)(2,1)S(1)}, bf16[512,2048]{1,0:T(8,128)(2,1)S(1)}, u32[]{:S(2)}, u32[]{:S(2)}) collective-permute-start(bf16[512,2048]{1,0:T(8,128)(2,1)S(1)} %copy-done.7), channel_id=1, source_target_pairs={{0,8},{8,16},{16,24},{24,0},{1,9},{9,17},{17,25},{25,1},{2,10},{10... | collective-permute-start | bytes 6291464 | tf_op jit(solution)/shard_map/ppermute | solution.py:89
  65.9 47.9 %collective-permute-start.1 = (bf16[512,2048]{1,0:T(8,128)(2,1)S(1)}, bf16[512,2048]{1,0:T(8,128)(2,1)}, u32[]{:S(2)}, u32[]{:S(2)}) collective-permute-start(bf16[512,2048]{1,0:T(8,128)(2,1)S(1)} %collective-permute-done), channel_id=1, source_target_pairs={{0,8},{8,16},{16,24},{24,0},{1,9},{9,17},{17,25},{25,1},{2,10},{10... | collective-permute-start | bytes 6291464 | tf_op jit(solution)/shard_map/ppermute | solution.py:89
  113.8 47.3 %collective-permute-start.2 = (bf16[512,2048]{1,0:T(8,128)(2,1)}, bf16[512,2048]{1,0:T(8,128)(2,1)}, u32[]{:S(2)}, u32[]{:S(2)}) collective-permute-start(bf16[512,2048]{1,0:T(8,128)(2,1)} %collective-permute-done.1), channel_id=1, source_target_pairs={{0,8},{8,16},{16,24},{24,0},{1,9},{9,17},{17,25},{25,1},{2,10},{10... | collective-permute-start | bytes 6291464 | tf_op jit(solution)/shard_map/ppermute | solution.py:89
  115.1 52.3 %copy-start.9 = (bf16[512,2048]{1,0:T(8,128)(2,1)S(1)}, bf16[512,2048]{1,0:T(8,128)(2,1)}, u32[]{:S(2)}) copy-start(bf16[512,2048]{1,0:T(8,128)(2,1)} %copy-done.8) | copy-start | bytes 6291460
  408.0 58.1 %all-gather.8.cloned.1.call-start = ((), (), s32[]{:S(2)}) async-start(), calls=%async_computation.2 | async-start | bytes 2359296 | tf_op jit(solution)/shard_map/all_gather | solution.py:152
  480.6 7.3 %copy-start.3 = (f32[2,4096,512]{1,2,0:T(8,128)}, f32[2,4096,512]{1,2,0:T(8,128)S(1)}, u32[]{:S(2)}) copy-start(f32[2,4096,512]{1,2,0:T(8,128)S(1)} %get-tuple-element.470) | copy-start | bytes 50331652 | tf_op jit(solution)/shard_map/while/body/eval_jaxpr/cond
  482.5 5.3 copy-start.6
  510.3 4.3 copy-start
  516.0 4.4 copy-start.1
  516.0 5.3 copy-start.4
  535.8 4.3 copy-start
  541.5 4.4 copy-start.1
  541.5 5.3 copy-start.4
  561.3 4.3 copy-start
  567.0 4.4 copy-start.1
  567.0 5.3 copy-start.4
  586.8 4.3 copy-start
  592.5 4.4 copy-start.1
  592.5 5.3 copy-start.4
  612.3 4.3 copy-start
  618.0 4.4 copy-start.1
  618.0 5.3 copy-start.4
  643.5 4.4 copy-start.1
  643.5 5.3 copy-start.4
  663.3 4.3 copy-start
  669.0 4.4 copy-start.1
  669.0 5.3 copy-start.4
  (13 other events, 29.3 us)
Sparse Core Ops, SparseCore 0:
  13.6 361.5 all-gather.3
  408.1 27.7 all-gather.5
  437.5 28.5 all-gather.7
